TPU v7x, 32 devices: a whole 2x2x4 slice. The times are simulated.
32 devices in a mesh: grp: 4 (over z), row: 4 (over y, core), col: 2 (over x).
Axes of the slice: x: 2, y: 2, z: 4, core: 2. Of those that a mesh axis runs over, the one named last changes fastest.
Arguments:
- tokens: bfloat16 [2048, 4608], P(('grp', 'row', 'col')), parts along dimension 0, may hold values from -6 to 6
- ln_gain: float32 [4608], replicated, may hold values from 0.1 to 1.9
- w_in: bfloat16 [4608, 12288], P('row', 'col'), may hold values from -0.09375 to 0.09375
- b_in: float32 [12288], P('col'), may hold values from -3 to 3
- w_out: bfloat16 [12288, 4608], P('col', 'row'), may hold values from -0.0546875 to 0.0546875
- b_out: float32 [4608], P('row'), may hold values from -3 to 3
Outputs:
- result: bfloat16 [2048, 4608], P(('grp', 'row', 'col')), parts along dimension 0
There are 4 independent parts, one for each index of `grp`. A program takes and returns all parts, laid end to end along the dimension named above; an argument that names none is the same for every part. Nothing has to cross between parts.
All inputs are finite; a program needn't handle non-finite values.
Results may differ from a plain program's by a relative error of at most 0.0095.
Values may be sent and summed in bfloat16 or wider, within the bound.
A program may use at most 128 MiB of HBM per device.

v0:
```python
import jax
import jax.numpy as jnp
from jax import lax
from jax.sharding import PartitionSpec as P


def local(tokens, ln_gain, w_in, b_in, w_out, b_out):
    values = tokens.astype(jnp.float32)
    row_mean = jnp.mean(values, axis=1, keepdims=True)
    centered = values - row_mean
    row_var = jnp.mean(centered * centered, axis=1, keepdims=True)
    normed = (centered * lax.rsqrt(row_var + 1e-06) * ln_gain).astype(jnp.bfloat16)
    own_cols = lax.all_to_all(normed, "row", split_axis=1, concat_axis=0, tiled=True)
    partial_pre = jnp.dot(
        lax.all_gather(own_cols, "col", axis=0, tiled=True),
        w_in,
        preferred_element_type=jnp.float32,
    )
    preact = lax.psum_scatter(partial_pre, "row", scatter_dimension=0, tiled=True) + b_in
    hidden = jax.nn.gelu(preact, approximate=False).astype(jnp.bfloat16)
    down_part = jnp.dot(
        lax.all_gather(hidden, "row", axis=0, tiled=True), w_out, preferred_element_type=jnp.float32
    )
    summed = lax.psum_scatter(
        down_part.astype(jnp.bfloat16), "col", scatter_dimension=0, tiled=True
    ).astype(jnp.float32)
    branch_out = (summed + b_out).astype(jnp.bfloat16)
    regrouped = lax.all_to_all(branch_out, "row", split_axis=0, concat_axis=1, tiled=True)
    return (values + regrouped.astype(jnp.float32)).astype(jnp.bfloat16)


def solution(mesh):
    in_specs = (
        P(("grp", "row", "col"), None),
        P(),
        P("row", "col"),
        P("col"),
        P("col", "row"),
        P("row"),
    )
    out_specs = P(("grp", "row", "col"), None)
    return jax.shard_map(local, mesh=mesh, in_specs=in_specs, out_specs=out_specs, check_vma=False)
```

profile of v0, /device:TPU:0, one launch (start us, length us, event | category | flops | bytes accessed | tf_op | source)
XLA Modules:
  0.0 273.9 jit_solution(3473818325535875934)
XLA Ops:
  6.5 0.0 all-gather.3.cloned.1.call-start
  6.5 1.2 convert_reduce_fusion
  7.8 1.4 fusion.12
  9.2 1.3 fusion.14
  10.6 13.7 %all_to_all.32 = bf16[64,4,1152]{2,0,1:T(8,128)(2,1)} all-to-all(bf16[64,4,1152]{2,0,1:T(8,128)(2,1)S(1)} %bitcast.19), channel_id=1, replica_groups=mesh['grp'=4,'row'=4,'col'=2] {'row'}, dimensions={1} | all-to-all | bytes 1179648 | tf_op jit(solution)/shard_map/all_to_all | solution.py:13
  24.3 0.0 all-gather.3.cloned.1.call-update
  24.3 0.0 reduce-scatter.3.cloned.1.call-start
  24.3 23.6 %all-gather.3.cloned.1.call-done = bf16[512,1152]{1,0:T(8,128)(2,1)} async-done(((bf16[256,1152]{1,0:T(8,128)(2,1)}), bf16[512,1152]{1,0:T(8,128)(2,1)}) %all-gather.3.cloned.1.call-update) | async-done | bytes 1179664 | tf_op jit(solution)/shard_map/all_gather | solution.py:15
  47.9 14.4 %fusion.16 = f32[512,6144]{1,0:T(8,128)} fusion(bf16[512,1152]{1,0:T(8,128)(2,1)} %all-gather.3.cloned.1.call-done, bf16[1152,6144]{1,0:T(8,128)(2,1)} %param.8), kind=kOutput, calls=%fused_computation.34 | convolution fusion | flops 7247757312 | bytes 27918336 | tf_op jit(solution)/shard_map/dot_general | solution.py:14
  62.3 0.0 copy-start.1
  62.3 0.0 reduce-scatter.3.cloned.1.call-update
  62.3 0.0 all-gather.5.cloned.1.call-start
  62.4 99.7 %reduce-scatter.3.cloned.1.call-done = f32[128,6144]{1,0:T(8,128)} async-done(((f32[512,6144]{1,0:T(8,128)}), f32[128,6144]{1,0:T(8,128)}) %reduce-scatter.3.cloned.1.call-update) | async-done | bytes 3145744 | tf_op jit(solution)/shard_map/reduce_scatter | solution.py:19
  162.1 0.0 copy-done.1
  162.1 8.8 %fusion.2 = bf16[128,6144]{1,0:T(8,128)(2,1)} fusion(f32[128,6144]{1,0:T(8,128)} %reduce-scatter.3.cloned.1.call-done, f32[6144]{0:T(1024)S(1)} %copy-done.1), kind=kLoop, calls=%fused_computation.3 | loop fusion | flops 51904512 | bytes 4743168 | tf_op jit(solution)/shard_map/convert_element_type | solution.py:20
  170.9 0.0 all-gather.5.cloned.1.call-update
  170.9 0.0 copy-start.2
  170.9 0.0 reduce-scatter.5.cloned.1.call-start
  171.0 46.4 %all-gather.5.cloned.1.call-done = bf16[512,6144]{1,0:T(8,128)(2,1)} async-done(((bf16[128,6144]{1,0:T(8,128)(2,1)}), bf16[512,6144]{1,0:T(8,128)(2,1)}) %all-gather.5.cloned.1.call-update) | async-done | bytes 6291472 | tf_op jit(solution)/shard_map/all_gather | solution.py:22
  217.4 13.6 %convolution_convert_fusion = bf16[512,1152]{1,0:T(8,128)(2,1)} fusion(bf16[512,6144]{1,0:T(8,128)(2,1)} %all-gather.5.cloned.1.call-done, bf16[6144,1152]{1,0:T(8,128)(2,1)} %param.10), kind=kOutput, calls=%fused_computation.19 | convolution fusion | flops 7248347136 | bytes 21626880 | tf_op jit(solution)/shard_map/dot_general | solution.py:21
  231.0 0.0 reduce-scatter.5.cloned.1.call-update
  231.0 0.0 copy-start
  231.0 22.0 %reduce-scatter.5.cloned.1.call-done = bf16[256,1152]{1,0:T(8,128)(2,1)} async-done(((bf16[512,1152]{1,0:T(8,128)(2,1)}), bf16[256,1152]{1,0:T(8,128)(2,1)}) %reduce-scatter.5.cloned.1.call-update) | async-done | bytes 589840 | tf_op jit(solution)/shard_map/reduce_scatter | solution.py:24
  253.0 0.0 copy-done.2
  253.0 1.2 add_convert_fusion
  254.1 12.1 %all_to_all.33 = bf16[4,64,1152]{2,1,0:T(8,128)(2,1)S(1)} all-to-all(bf16[4,64,1152]{2,1,0:T(8,128)(2,1)S(1)} %bitcast.20), channel_id=1, replica_groups=mesh['grp'=4,'row'=4,'col'=2] {'row'}, dimensions={0} | all-to-all | bytes 1179648 | tf_op jit(solution)/shard_map/all_to_all | solution.py:28
  266.2 0.1 convert_bitcast_fusion
  266.3 0.1 copy.14
  266.4 0.0 copy-done
  266.4 0.9 fusion.15
  (3 shorter events, 0.1 us)
Async XLA Ops:
  6.5 41.3 %all-gather.3.cloned.1.call-start = ((), (), s32[]{:S(2)}) async-start(), calls=%async_computation.4 | async-start | bytes 1769472 | tf_op jit(solution)/shard_map/all_gather | solution.py:15
  24.3 137.8 %reduce-scatter.3.cloned.1.call-start = ((), (), s32[]{:S(2)}) async-start(), calls=%async_computation.5 | async-start | bytes 15728640 | tf_op jit(solution)/shard_map/reduce_scatter | solution.py:19
  62.3 99.8 %copy-start.1 = (f32[6144]{0:T(1024)S(1)}, f32[6144]{0:T(1024)}, u32[]{:S(2)}) copy-start(f32[6144]{0:T(1024)} %param.9) | copy-start | bytes 73732
  62.3 155.1 %all-gather.5.cloned.1.call-start = ((), (), s32[]{:S(2)}) async-start(), calls=%async_computation.6 | async-start | bytes 7864320 | tf_op jit(solution)/shard_map/all_gather | solution.py:22
  170.9 82.1 %copy-start.2 = (f32[1152]{0:T(1024)S(1)}, f32[1152]{0:T(1024)}, u32[]{:S(2)}) copy-start(f32[1152]{0:T(1024)} %param.11) | copy-start | bytes 13828
  170.9 82.0 %reduce-scatter.5.cloned.1.call-start = ((), (), s32[]{:S(2)}) async-start(), calls=%async_computation.7 | async-start | bytes 1769472 | tf_op jit(solution)/shard_map/reduce_scatter | solution.py:24
  231.0 35.4 %copy-start = (bf16[64,4608]{1,0:T(8,128)(2,1)S(1)}, bf16[64,4608]{1,0:T(8,128)(2,1)}, u32[]{:S(2)}) copy-start(bf16[64,4608]{1,0:T(8,128)(2,1)} %param.6) | copy-start | bytes 1769476
Sparse Core Ops, SparseCore 0:
  24.4 23.4 all-gather.2
  62.5 99.6 reduce-scatter.2
  171.0 46.3 all-gather.4
  231.1 21.8 reduce-scatter.4
where the time goes:
time: 274 us
  waiting for transfers between devices  192 us (70%)
  matrix products  28 us (10%)
  blocking collectives  25.8 us (9%)
  other arithmetic  14.9 us (5%)
  between operations  13.2 us (5%)
    reduce_scatter x1, waiting for transfers between devices, local(): lax.psum_scatter(partial_pre, 'row', scatter_dimension=0, tiled=True) + b_in  99.7 us
    all_gather x1, waiting for transfers between devices, local(): lax.all_gather(hidden, 'row', axis=0, tiled=True)  46.4 us
    all_gather x1, waiting for transfers between devices, local(): lax.all_gather(own_cols, 'col', axis=0, tiled=True)  23.6 us
    reduce_scatter x1, waiting for transfers between devices, local(): lax.psum_scatter(down_part.astype(jnp.bfloat16), 'col', scatter_dimension...  22 us
    dot_general x1, matrix products, local(): jnp.dot(lax.all_gather(own_cols, 'col', axis=0, tiled=True), w_in, prefer...  14.4 us
    all_to_all x1, blocking collectives, local(): lax.all_to_all(normed, 'row', split_axis=1, concat_axis=0, tiled=True)  13.7 us
    dot_general x1, matrix products, local(): jnp.dot(lax.all_gather(hidden, 'row', axis=0, tiled=True), w_out, preferr...  13.6 us
    all_to_all x1, blocking collectives, local(): lax.all_to_all(branch_out, 'row', split_axis=0, concat_axis=1, tiled=True)  12.1 us
  transfers between devices with their start and end apart: 4, of which 4 were waited for; matrix products, arithmetic and copies ran while one was open for 0% of the time, Pallas kernels for 0%

commit v1 on v0

--- a/solution.py
+++ b/solution.py
@@ -12,7 +12,9 @@
     normed = (centered * lax.rsqrt(row_var + 1e-06) * ln_gain).astype(jnp.bfloat16)
     own_cols = lax.all_to_all(normed, "row", split_axis=1, concat_axis=0, tiled=True)
     partial_pre = jnp.dot(
-        lax.all_gather(own_cols, "col", axis=0, tiled=True),
+        jnp.concatenate(
+            lax.all_to_all(jnp.stack([own_cols] * lax.axis_size("col")), "col", 0, 0), axis=0
+        ),
         w_in,
         preferred_element_type=jnp.float32,
     )

time: 274 us -> 267 us (0.974)
  waiting for transfers between devices: 192 us -> 168 us
  blocking collectives: 25.8 us -> 43.3 us
    all_gather x1 -> x0, waiting for transfers between devices: 23.6 us -> none  [local(): lax.all_gather(own_cols, 'col', axis=0, tiled=True)]
    all_to_all x0 -> x1, blocking collectives: none -> 17.7 us  [local(): lax.all_to_all(jnp.stack([own_cols] * lax.axis_size('col')), 'col', 0, 0)]
  transfers between devices with their start and end apart: 4 -> 3, of which waited for: 4 -> 3; matrix products, arithmetic and copies ran while one was open for 0% -> 0% of each run, Pallas kernels for 0% -> 0%
where the time goes in v1:
time: 267 us
  waiting for transfers between devices  168 us (63%)
  blocking collectives  43.3 us (16%)
  matrix products  27.7 us (10%)
  other arithmetic  15 us (6%)
  between operations  13.2 us (5%)
    reduce_scatter x1, waiting for transfers between devices, local(): lax.psum_scatter(partial_pre, 'row', scatter_dimension=0, tiled=True) + b_in  99.1 us
    all_gather x1, waiting for transfers between devices, local(): lax.all_gather(hidden, 'row', axis=0, tiled=True)  46.4 us
    reduce_scatter x1, waiting for transfers between devices, local(): lax.psum_scatter(down_part.astype(jnp.bfloat16), 'col', scatter_dimension...  22 us
    all_to_all x1, blocking collectives, local(): lax.all_to_all(jnp.stack([own_cols] * lax.axis_size('col')), 'col', 0, 0)  17.7 us
    dot_general x1, matrix products, local(): jnp.dot(jnp.concatenate(lax.all_to_all(jnp.stack([own_cols] * lax.axis_si...  14.2 us
    all_to_all x1, blocking collectives, local(): lax.all_to_all(normed, 'row', split_axis=1, concat_axis=0, tiled=True)  13.6 us
    dot_general x1, matrix products, local(): jnp.dot(lax.all_gather(hidden, 'row', axis=0, tiled=True), w_out, preferr...  13.6 us
    all_to_all x1, blocking collectives, local(): lax.all_to_all(branch_out, 'row', split_axis=0, concat_axis=1, tiled=True)  12.1 us
  transfers between devices with their start and end apart: 3, of which 3 were waited for; matrix products, arithmetic and copies ran while one was open for 0% of the time, Pallas kernels for 0%

profile of v1, /device:TPU:0, one launch (start us, length us, event | category | flops | bytes accessed | tf_op | source)
XLA Modules:
  0.0 267.0 jit_solution(5000225059019979598)
XLA Ops:
  6.5 0.0 reduce-scatter.3.cloned.1.call-start
  6.5 1.2 convert_reduce_fusion
  7.8 1.4 fusion.12
  9.2 1.3 fusion.14
  10.6 13.6 %all_to_all.34 = bf16[64,4,1152]{2,0,1:T(8,128)(2,1)S(1)} all-to-all(bf16[64,4,1152]{2,0,1:T(8,128)(2,1)S(1)} %bitcast.20), channel_id=1, replica_groups=mesh['grp'=4,'row'=4,'col'=2] {'row'}, dimensions={1} | all-to-all | bytes 1179648 | tf_op jit(solution)/shard_map/all_to_all | solution.py:13
  24.1 0.1 pad_maximum_fusion
  24.3 17.7 %all_to_all.35 = bf16[2,256,1152]{2,1,0:T(8,128)(2,1)S(1)} all-to-all(bf16[2,256,1152]{2,1,0:T(8,128)(2,1)S(1)} %pad_maximum_fusion), channel_id=1, replica_groups=mesh['grp'=4,'row'=4,'col'=2] {'col'}, dimensions={0} | all-to-all | bytes 2359296 | tf_op jit(solution)/shard_map/all_to_all | solution.py:16
  41.9 14.2 %fusion.16 = f32[512,6144]{1,0:T(8,128)} fusion(bf16[512,1152]{1,0:T(8,128)(2,1)S(1)} %bitcast.22, bf16[1152,6144]{1,0:T(8,128)(2,1)} %param.8), kind=kOutput, calls=%fused_computation.35 | convolution fusion | flops 7247757312 | bytes 27918336 | tf_op jit(solution)/shard_map/dot_general | solution.py:14
  56.1 0.0 copy-start.1
  56.1 0.0 reduce-scatter.3.cloned.1.call-update
  56.1 0.0 all-gather.2.cloned.1.call-start
  56.2 99.1 %reduce-scatter.3.cloned.1.call-done = f32[128,6144]{1,0:T(8,128)} async-done(((f32[512,6144]{1,0:T(8,128)}), f32[128,6144]{1,0:T(8,128)}) %reduce-scatter.3.cloned.1.call-update) | async-done | bytes 3145744 | tf_op jit(solution)/shard_map/reduce_scatter | solution.py:21
  155.3 0.0 copy-done.1
  155.3 8.8 %fusion.2 = bf16[128,6144]{1,0:T(8,128)(2,1)} fusion(f32[128,6144]{1,0:T(8,128)} %reduce-scatter.3.cloned.1.call-done, f32[6144]{0:T(1024)S(1)} %copy-done.1), kind=kLoop, calls=%fused_computation.3 | loop fusion | flops 51904512 | bytes 4743168 | tf_op jit(solution)/shard_map/convert_element_type | solution.py:22
  164.1 0.0 all-gather.2.cloned.1.call-update
  164.1 0.0 copy-start.2
  164.1 0.0 reduce-scatter.5.cloned.1.call-start
  164.2 46.4 %all-gather.2.cloned.1.call-done = bf16[512,6144]{1,0:T(8,128)(2,1)} async-done(((bf16[128,6144]{1,0:T(8,128)(2,1)}), bf16[512,6144]{1,0:T(8,128)(2,1)}) %all-gather.2.cloned.1.call-update) | async-done | bytes 6291472 | tf_op jit(solution)/shard_map/all_gather | solution.py:24
  210.6 13.6 %convolution_convert_fusion = bf16[512,1152]{1,0:T(8,128)(2,1)} fusion(bf16[512,6144]{1,0:T(8,128)(2,1)} %all-gather.2.cloned.1.call-done, bf16[6144,1152]{1,0:T(8,128)(2,1)} %param.10), kind=kOutput, calls=%fused_computation.19 | convolution fusion | flops 7248347136 | bytes 21626880 | tf_op jit(solution)/shard_map/dot_general | solution.py:23
  224.2 0.0 reduce-scatter.5.cloned.1.call-update
  224.2 0.0 copy-start
  224.2 22.0 %reduce-scatter.5.cloned.1.call-done = bf16[256,1152]{1,0:T(8,128)(2,1)} async-done(((bf16[512,1152]{1,0:T(8,128)(2,1)}), bf16[256,1152]{1,0:T(8,128)(2,1)}) %reduce-scatter.5.cloned.1.call-update) | async-done | bytes 589840 | tf_op jit(solution)/shard_map/reduce_scatter | solution.py:26
  246.2 0.0 copy-done.2
  246.2 1.2 add_convert_fusion
  247.3 12.1 %all_to_all.36 = bf16[4,64,1152]{2,1,0:T(8,128)(2,1)S(1)} all-to-all(bf16[4,64,1152]{2,1,0:T(8,128)(2,1)S(1)} %bitcast.21), channel_id=1, replica_groups=mesh['grp'=4,'row'=4,'col'=2] {'row'}, dimensions={0} | all-to-all | bytes 1179648 | tf_op jit(solution)/shard_map/all_to_all | solution.py:30
  259.4 0.1 convert_bitcast_fusion
  259.5 0.1 copy.14
  259.6 0.0 copy-done
  259.6 0.9 fusion.15
  (3 shorter events, 0.1 us)
Async XLA Ops:
  6.5 148.7 %reduce-scatter.3.cloned.1.call-start = ((), (), s32[]{:S(2)}) async-start(), calls=%async_computation.5 | async-start | bytes 15728640 | tf_op jit(solution)/shard_map/reduce_scatter | solution.py:21
  56.1 99.2 %copy-start.1 = (f32[6144]{0:T(1024)S(1)}, f32[6144]{0:T(1024)}, u32[]{:S(2)}) copy-start(f32[6144]{0:T(1024)} %param.9) | copy-start | bytes 73732
  56.1 154.5 %all-gather.2.cloned.1.call-start = ((), (), s32[]{:S(2)}) async-start(), calls=%async_computation.6 | async-start | bytes 7864320 | tf_op jit(solution)/shard_map/all_gather | solution.py:24
  164.1 82.1 %copy-start.2 = (f32[1152]{0:T(1024)S(1)}, f32[1152]{0:T(1024)}, u32[]{:S(2)}) copy-start(f32[1152]{0:T(1024)} %param.11) | copy-start | bytes 13828
  164.1 82.0 %reduce-scatter.5.cloned.1.call-start = ((), (), s32[]{:S(2)}) async-start(), calls=%async_computation.7 | async-start | bytes 1769472 | tf_op jit(solution)/shard_map/reduce_scatter | solution.py:26
  224.2 35.4 %copy-start = (bf16[64,4608]{1,0:T(8,128)(2,1)S(1)}, bf16[64,4608]{1,0:T(8,128)(2,1)}, u32[]{:S(2)}) copy-start(bf16[64,4608]{1,0:T(8,128)(2,1)} %param.6) | copy-start | bytes 1769476
Sparse Core Ops, SparseCore 0:
  56.2 98.9 reduce-scatter.2
  164.2 46.3 all-gather.1
  224.3 21.8 reduce-scatter.4
